TPU v7x, 128 devices: a whole 4x4x4 slice. The times are simulated.
128 devices in a mesh: part: 1, row: 2 (over core), col: 64 (over z, y, x).
Axes of the slice: x: 4, y: 4, z: 4, core: 2. Of those that a mesh axis runs over, the one named last changes fastest.
Arguments:
- ratings: float32 [4096, 32768], P(('part', 'row'), 'col')
- mask: int32 [4096, 32768], P(('part', 'row'), 'col')
- v_init: float32 [32768, 50], P(('part', 'col'))
Outputs:
- output 1: float32 [4096, 50], P(('part', 'row', 'col'))
- output 2: float32 [32768, 50], P(('part', 'col', 'row'))
All inputs are finite; a program needn't handle non-finite values.
Results may differ from a plain program's by a relative error of at most 0.001.
Values are sent between devices in bfloat16 or wider.
A program may use at most 1 GiB of HBM per device.

v0:
```python
import jax
import jax.numpy as jnp
from jax import lax
from jax.experimental import pallas as pl
from jax.experimental.pallas import tpu as pltpu
from jax.sharding import PartitionSpec as P

RIDGE_WEIGHT = 0.05
WIDTH = 50
ROWS = 56
TRI = 1280
LANES = 128


def tri_off(j):
    return j * WIDTH - j * (j - 1) // 2


def outer_tile(vt, dst):
    lanes = vt.shape[1]
    for j in range(WIDTH):
        rows = WIDTH - j
        dst[tri_off(j):tri_off(j) + rows, :] = vt[j:WIDTH, :] * vt[j:j + 1, :]


def solve_tiles(g_ref, rhs_ref, facs, inv, sol, ready=None):
    groups = [slice(i * LANES, (i + 1) * LANES) for i in range(len(facs))]
    for pan in range(7):
        first = 8 * pan
        rows = ROWS - first
        count = min(8, WIDTH - first)
        if ready is not None:
            ready(pan)
        ids = lax.broadcasted_iota(jnp.int32, (rows, LANES), 0)

        def panel(here):
            accs = []
            for c in range(count):
                j = first + c
                start = tri_off(j) - c
                if j < WIDTH - 1:
                    raw = g_ref[start:start + rows, here]
                else:
                    raw = jnp.broadcast_to(g_ref[tri_off(j):tri_off(j) + 1, here], (rows, LANES))
                col = jnp.where(ids < WIDTH - first, raw, 0.0)
                col = jnp.where(ids == c, col + RIDGE_WEIGHT, col)
                accs.append(jnp.where(ids == WIDTH - first, rhs_ref[j:j + 1, here], col))
            return accs

        def update(fac, k, accs):
            base = pl.multiple_of(k * ROWS, 8)
            left = fac[pl.ds(base + first, rows), :]
            return [acc - left * fac[pl.ds(base + first + c, 1), :] for c, acc in enumerate(accs)]

        if not pan:
            parts = [panel(here) for here in groups]
        elif len(groups) * count * rows <= 48 * 8:
            parts = lax.fori_loop(
                0, first, lambda k, parts: [update(fac, k, accs) for fac, accs in zip(facs, parts)],
                [panel(here) for here in groups], unroll=2,
            )
        else:
            parts = []
            for here, fac in zip(groups, facs):
                parts.append(lax.fori_loop(0, first, lambda k, accs: update(fac, k, accs), panel(here), unroll=2))
        parts = [list(accs) for accs in parts]
        for c in range(count):
            j = first + c
            for here, fac, accs in zip(groups, facs, parts):
                diag = accs[c][c:c + 1, :]
                root = lax.rsqrt(diag)
                root = root * (1.5 - 0.5 * (diag * root) * root)
                inv[j:j + 1, here] = root
                col = accs[c] * root
                fac[pl.ds(j * ROWS + first, rows), :] = col
                for later in range(c + 1, count):
                    accs[later] = accs[later] - col * col[later:later + 1, :]
    for here in groups:
        sol[48:56, here] = jnp.zeros((8, LANES), jnp.float32)
    for pan in reversed(range(7)):
        first = 8 * pan
        count = min(8, WIDTH - first)
        lefts = []
        for here, fac in zip(groups, facs):
            left = []
            for c in range(count):
                j = first + c
                val = fac[j * ROWS + WIDTH:j * ROWS + WIDTH + 1, :]
                if pan < 6:
                    dot = fac[j * ROWS + first + 8:j * ROWS + ROWS, :] * sol[first + 8:ROWS, here]
                    val = val - jnp.sum(dot, axis=0, keepdims=True)
                left.append(val)
            lefts.append(left)
        for c in reversed(range(count)):
            j = first + c
            for here, fac, left in zip(groups, facs, lefts):
                got = left[c] * inv[j:j + 1, here]
                sol[j:j + 1, here] = got
                for early in range(c):
                    row = (first + early) * ROWS + j
                    left[early] = left[early] - fac[row:row + 1, :] * got


def item_solve_kernel(g_hbm, w_ref, out_ref, w_out, gram, inv, sol, sems, *facs):
    copies = []
    for i, (start, stop) in enumerate(((0, 384), (TRI, gram.shape[0]), (384, 688), (688, TRI))):
        copy = pltpu.make_async_copy(g_hbm.at[start:stop], gram.at[start:stop], sems.at[i])
        copy.start()
        copies.append(copy)
    w_out[...] = w_ref[...]

    def ready(pan):
        for copy in (copies[:2], copies[2:3], copies[3:], [], [], [], [])[pan]:
            copy.wait()

    solve_tiles(gram, gram.at[TRI:gram.shape[0]], facs, inv, sol, ready)
    out_ref[...] = sol[:WIDTH, :]


def solve_items(packed, w_own):
    n = packed.shape[1]
    vmem_spec = pl.BlockSpec(memory_space=pltpu.VMEM)
    return pl.pallas_call(
        item_solve_kernel,
        out_shape=(jax.ShapeDtypeStruct((WIDTH, n), jnp.float32), jax.ShapeDtypeStruct(w_own.shape, jnp.float32)),
        in_specs=[pl.BlockSpec(memory_space=pl.ANY), vmem_spec],
        out_specs=(vmem_spec, vmem_spec),
        scratch_shapes=[
            pltpu.VMEM(packed.shape, jnp.float32),
            pltpu.VMEM((ROWS, n), jnp.float32),
            pltpu.VMEM((ROWS, n), jnp.float32),
            pltpu.SemaphoreType.DMA((4,)),
        ] + [pltpu.VMEM((WIDTH * ROWS, LANES), jnp.float32)] * (n // LANES),
    )(packed, w_own)


PACK = 1344
FULL = 1408
SIDE = 4
HALF = PACK // 2
CUT = 384


def dot_cols(left, right):
    return lax.dot_general(left, right, (((1,), (1,)), ((), ())), preferred_element_type=jnp.float32)


def als_kernel(
    rate_hbm, mask_hbm, v_hbm, w_hbm, item_hbm,
    rate, mask, v_raw, mqs, hop, rhs, vt_all, o_all, tmp, gram, home, unit, rel, got, tot, acc, flat, fin,
    fac, inv, sol, w_new, pack, w_all, wt, wb, part, swap_got, item_sum,
    v_sem, load_sem, v_send, v_recv, m_send, m_recv, hop_send, hop_recv, fwd_send, own_sem,
    rel_send, rel_recv, got_send, got_recv, fin_send, fin_recv, w_send, w_recv, w_sem, x_send, x_recv, out_sem, y_in, z_in,
):
    items = v_raw.shape[1]
    count = w_all.shape[0]
    col = lax.axis_index("col")
    row = lax.axis_index("row")
    other = {"row": 1 - row}
    x = lax.rem(col, SIDE)
    y = lax.rem(col // SIDE, SIDE)
    z = col // (SIDE * SIDE)

    def turn(pos, step):
        return lax.rem(pos + step, SIDE)

    def x_peer(step):
        return {"col": col - x + turn(x, step)}

    def y_peer(step):
        return {"col": col + SIDE * (turn(y, step) - y)}

    def z_peer(step):
        return {"col": col + SIDE * SIDE * (turn(z, step) - z)}

    def send(src, dst, send_sem, recv_sem, peer):
        return pltpu.make_async_remote_copy(
            src_ref=src, dst_ref=dst, send_sem=send_sem, recv_sem=recv_sem,
            device_id=peer, device_id_type=pl.DeviceIdType.MESH,
        )

    def signal(sem, peer):
        pl.semaphore_signal(sem, inc=1, device_id=peer, device_id_type=pl.DeviceIdType.MESH)

    def start(copies):
        for copy in copies:
            copy.start()

    def take(ref, sem):
        pltpu.make_async_copy(ref, ref, sem).wait()

    barrier = pltpu.get_barrier_semaphore()
    peers = [peer(step) for step in (1, 2, 3) for peer in (x_peer, y_peer, z_peer)] + [other]
    for peer in peers:
        signal(barrier, peer)

    owners = [turn(z, 2), turn(z, 1), turn(z, 3), z]
    block = rate.shape[1]
    v_load = pltpu.make_async_copy(v_hbm, v_raw, v_sem)
    v_load.start()
    loads = []
    for k, owner in enumerate(owners):
        rows = pl.ds(pl.multiple_of(owner * block, block), block)
        pair = [
            pltpu.make_async_copy(rate_hbm.at[rows], rate.at[k], load_sem.at[k]),
            pltpu.make_async_copy(mask_hbm.at[rows], mask.at[k], load_sem.at[k]),
        ]
        loads.append(pair)
    start(loads[0])

    def cast_chunk(k):
        def cast_step(i, carry):
            rows = pl.ds(pl.multiple_of(i * 128, 128), 128)
            seen = mask[k, rows, :]
            mqs[k, i, :, :, 0] = seen.astype(jnp.float32).astype(jnp.bfloat16).reshape(SIDE, 2, 16, items)
            rated = jnp.where(seen != 0, rate[k, rows, :], 0.0)
            mqs[k, i, :, :, 1] = rated.astype(jnp.bfloat16).reshape(SIDE, 2, 16, items)
            return carry

        lax.fori_loop(0, SIDE, cast_step, 0)

    def axis_peer(c, step):
        return y_peer(step) if c else x_peer(step)

    def share(s, c, pos):
        return mqs.at[(0, 2, 1, 3)[s], pos, :, 1] if c else mqs.at[s, :, pos, 0]

    def columns(slot):
        return slice(slot * items, (slot + 1) * items)

    m_copies, own_copies, hops, passes = [], [], [], []
    for s in range(4):
        m_copies.append([])
        own_copies.append([])
        hops.append([])
        passes.append([])
        for c, pos in enumerate((x, y)):
            for m, step in enumerate((1, 3)):
                hops[s].append(send(
                    share(s, c, turn(pos, 2)).at[:, m], hop.at[s, c, m],
                    hop_send, hop_recv.at[s], axis_peer(c, step),
                ))
                m_copies[s].append(send(
                    share(s, c, turn(pos, step)), rhs.at[s, c, :, :, :, columns(3 * c + step)],
                    m_send, m_recv.at[s], axis_peer(c, step),
                ))
                passes[s].append(send(
                    hop.at[s, c, m], rhs.at[s, c, :, m, :, columns(3 * c + 2)],
                    fwd_send, m_recv.at[s], axis_peer(c, step),
                ))
            own_copies[s].append(pltpu.make_async_copy(
                share(s, c, pos), rhs.at[s, c, :, :, :, columns(0)], own_sem.at[s]
            ))

    def pass_on(s):
        take(hop.at[s], hop_recv.at[s])
        start(passes[s])

    def half_columns(slot, side):
        return pl.ds(pl.multiple_of(slot * items + side * (items // 2), items // 2), items // 2)

    v_copies, v_swaps = [], []
    for d in (1, 3, 2):
        for axis in range(2):
            slot = 3 * axis + d
            v_copies.append(send(
                vt_all.at[:, half_columns(0, row)], vt_all.at[:, half_columns(slot, row)],
                v_send.at[0], v_recv.at[d], axis_peer(axis, d),
            ))
            v_swaps.append(send(
                vt_all.at[:, half_columns(slot, row)], vt_all.at[:, half_columns(slot, row)],
                v_send.at[1], v_recv.at[0], other,
            ))

    tmp[48:64, :] = jnp.zeros((16, items), jnp.float32)
    v_load.wait()
    tmp[0:WIDTH, :] = v_raw[...]
    vt_all[:, 0:items] = tmp[0:64, :].astype(jnp.bfloat16)
    take(rate.at[0:2], load_sem.at[0])
    for k in range(1, 4):
        start(loads[k])
    cast_chunk(0)
    pl.semaphore_wait(barrier, len(peers))
    start(v_copies)
    start(hops[0])
    start(m_copies[0])
    for step in (1, 2, 3):
        signal(y_in, y_peer(step))
    for k in range(1, 4):
        take(rate.at[0:2], load_sem.at[k])
        cast_chunk(k)
    for s in range(4):
        start(own_copies[s])
    for s in range(4):
        rhs[s, 0, :, :, :, 4 * items:7 * items] = jnp.zeros((4, 2, 16, 3 * items), jnp.bfloat16)
        rhs[s, 1, :, :, :, items:4 * items] = jnp.zeros((4, 2, 16, 3 * items), jnp.bfloat16)
    tmp[1272:1280, :] = jnp.zeros((8, items), jnp.float32)

    def outer_step(slot, carry):
        cols = pl.ds(pl.multiple_of(slot * items, items), items)
        outer_tile(vt_all[:, cols].astype(jnp.float32), tmp)
        o_all[:, cols] = tmp[...].astype(jnp.bfloat16)
        return carry

    lax.fori_loop(0, 1, outer_step, 0)
    for i, d in enumerate((1, 3, 2)):
        take(vt_all.at[:, 0:items], v_recv.at[d])
        start(v_swaps[2 * i:2 * i + 2])
    pass_on(0)
    start(hops[1])
    start(m_copies[1])
    start(hops[2])
    pl.semaphore_wait(y_in, 3)
    for step in (1, 2, 3):
        signal(z_in, z_peer(step))

    def users_of(s, m, cols):
        return rhs[s, :, :, m, :, cols].reshape(128, cols.stop - cols.start)

    near, far = slice(0, items), slice(items, 7 * items)
    def own_part(s):
        take(hop.at[s], own_sem.at[s])

        def near_step(i, carry):
            rows = pl.ds(pl.multiple_of(i * 640, 640), 640)
            home[s, rows, :] = dot_cols(o_all[rows, near], users_of(s, 0, near))
            return carry

        home[s, TRI:PACK, :] = dot_cols(vt_all[:, near], users_of(s, 1, near))
        lax.fori_loop(0, 2, near_step, 0)
    own_part(0)
    take(vt_all.at[:, 0:3 * items], v_recv.at[0])
    lax.fori_loop(1, 7, outer_step, 0)

    low = lax.broadcasted_iota(jnp.int32, (HALF, 128), 1) < 64
    pieces = (slice(0, CUT), slice(CUT, HALF))
    ways = (1, 3)

    def partial(s, dst, p):
        rows = pieces[p]
        for rows in (rows, slice(HALF + rows.start, min(HALF + rows.stop, TRI))):
            dst[rows, :] = home[s, rows, :] + dot_cols(o_all[rows, far], users_of(s, 0, far))
        if p:
            dst[TRI:PACK, :] = home[s, TRI:PACK, :] + dot_cols(vt_all[:, far], users_of(s, 1, far))

    def arrived(s):
        take(mqs.at[0, 0:3], m_recv.at[s])

    def pack_units(s, p):
        rows = pieces[p]
        partial(s, gram, p)
        here = low[:rows.stop - rows.start]
        top, bottom = gram[rows, :], gram[HALF + rows.start:HALF + rows.stop, :]
        unit[s, 0, rows, :] = jnp.where(here, top, pltpu.roll(bottom, 64, 1))
        unit[s, 1, rows, :] = jnp.where(here, pltpu.roll(top, 64, 1), bottom)

    arrived(0)
    for p, rows in enumerate(pieces):
        pack_units(0, p)
        for c in range(2):
            send(unit.at[0, c, rows], rel.at[c, rows], rel_send, rel_recv.at[p], z_peer(ways[c])).start()
    pass_on(1)
    start(m_copies[2])
    start(hops[3])
    own_part(1)
    pass_on(2)
    start(m_copies[3])
    own_part(2)
    arrived(1)
    for p, rows in enumerate(pieces):
        pack_units(1, p)
        take(rel.at[:, rows], rel_recv.at[p])
        for c in range(2):
            unit[1, c, rows, :] = unit[1, c, rows, :] + rel[c, rows, :]
            send(unit.at[1, c, rows], got.at[0, c, rows], got_send, got_recv.at[0], z_peer(ways[c])).start()
    pass_on(3)
    arrived(2)
    for p, rows in enumerate(pieces):
        pack_units(2, p)
        for c in range(2):
            send(
                unit.at[2, c, rows], got.at[1, c, rows], got_send, got_recv.at[1 + p], z_peer(ways[1 - c])
            ).start()
    own_part(3)
    arrived(3)
    for p in range(2):
        partial(3, tot, p)
    acc[PACK:FULL, :] = jnp.zeros((FULL - PACK, 128), jnp.float32)
    take(got.at[0], got_recv.at[0])
    pl.semaphore_wait(z_in, 3)
    for p, rows in enumerate(pieces):
        size = rows.stop - rows.start
        take(got.at[1, :, rows], got_recv.at[1 + p])
        sum_a = got[0, 0, rows] + got[1, 0, rows]
        sum_b = got[0, 1, rows] + got[1, 1, rows]
        here = low[:size]
        at = 2 * rows.start
        acc[at:at + size, :] = tot[rows, :] + jnp.where(here, sum_a, pltpu.roll(sum_b, 64, 1))
        acc[at + size:at + 2 * size, :] = (
            tot[HALF + rows.start:HALF + rows.stop, :] + jnp.where(here, pltpu.roll(sum_a, 64, 1), sum_b)
        )
        cols = slice(at, FULL if p else 2 * CUT)
        for i in range(cols.start // 128, cols.stop // 128):
            flat[:, i * 128:(i + 1) * 128] = acc[i * 128:(i + 1) * 128, :].T
        for d in (2, 1, 3):
            for c, pos in enumerate((y, x)):
                users = pl.ds(pl.multiple_of(64 * c + 16 * turn(pos, d), 16), 16)
                send(
                    flat.at[users, cols], fin.at[c, d - 1, :, cols], fin_send, fin_recv, axis_peer(1 - c, d)
                ).start()
    take(fin, fin_recv)

    zeros = jnp.zeros((96, 128), jnp.float32)
    for i in range(FULL // 128):
        cols = slice(i * 128, (i + 1) * 128)
        mine = [zeros]
        for c, pos in ((1, x), (0, y)):
            rows = pl.ds(pl.multiple_of(64 * c + 16 * pos, 16), 16)
            mine.insert(0, flat[rows, cols] + fin[c, 0, :, cols] + fin[c, 1, :, cols] + fin[c, 2, :, cols])
        acc[cols, :] = jnp.concatenate(mine, axis=0).T
    for rows in pieces:
        size = rows.stop - rows.start
        tot[rows, :] = acc[2 * rows.start:2 * rows.start + size, :]
        tot[HALF + rows.start:HALF + rows.stop, :] = acc[2 * rows.start + size:2 * rows.stop, :]
    solve_tiles(tot, tot.at[TRI:PACK], [fac], inv, sol)
    turned = jnp.concatenate([sol[...], jnp.zeros((72, 128), jnp.float32)], axis=0).T
    lane = lax.broadcasted_iota(jnp.int32, (16, 128), 1)
    pack[...] = jnp.where(lane < 64, turned[:16], pltpu.roll(turned[16:32], 64, 1)).astype(jnp.bfloat16)

    plane = SIDE * SIDE

    place = col - z * plane
    w_own = pltpu.make_async_copy(pack, w_all.at[col], w_recv.at[0])
    w_own.start()
    for t, turned_by in enumerate((0, 1, 3, 2)):
        base = turn(z, turned_by) * plane

        def send_step(i, carry):
            target = place + i
            target = base + jnp.where(target < plane, target, target - plane)
            send(pack, w_all.at[col], w_send, w_recv.at[(0, 2, 1, 3)[t]], {"col": target}).start()
            return carry

        lax.fori_loop(0 if t else 1, plane, send_step, 0)
    w_new[...] = turned[:32, :WIDTH]
    w_out = pltpu.make_async_copy(w_new, w_hbm, w_sem)
    w_out.start()

    users = 16 * count
    step = 16 * plane
    tall = tmp.at[:, 0:step]
    tall[1272:1280, :] = jnp.zeros((8, step), jnp.float32)

    def plane_step(t, carry):
        k = 3 - 2 * t + 3 * (t // 2)
        owner = turn(z, t + (t // 2) * (5 - 2 * t))

        take(w_all.at[0:plane], w_recv.at[t])
        for i in range(step // 128):
            rows = w_all[pl.ds(owner * plane + 8 * i, 8)].reshape(128, 128)
            wt[:, i * 128:(i + 1) * 128] = rows.astype(jnp.float32).T

        def colour_step(c, carry):
            vals = wt[pl.ds(pl.multiple_of(64 * c, 64), 64), :]
            cols = pl.ds(pl.multiple_of(c * users + k * step, step), step)
            wb[:, cols] = vals.astype(jnp.bfloat16)
            outer_tile(vals, tall)
            o_all[:, cols] = tall[...].astype(jnp.bfloat16)
            return carry

        lax.fori_loop(0, 2, colour_step, 0)
        return carry

    lax.fori_loop(0, SIDE, plane_step, 0)
    half = items // 2

    def item_rows(side, left, m):
        cols = pl.ds(pl.multiple_of(side * half, half), half)
        total = None
        for c in range(2):
            right = mqs[:, :, :, c, m, :, cols].reshape(users, half)
            term = jnp.dot(left(c), right, preferred_element_type=jnp.float32)
            total = term if total is None else total + term
        return total

    def rhs_rows(side):
        return item_rows(side, lambda c: wb[:, c * users:(c + 1) * users], 1)

    def gram_rows(side, rows):
        return item_rows(side, lambda c: o_all[rows, c * users:(c + 1) * users], 0)

    def swap_copy(i, rows):
        return send(part.at[rows], swap_got.at[rows], x_send, x_recv.at[i], other)

    def finish(i, rows, val):
        swap_copy(i, rows).wait_recv()
        item_sum[rows, :] = val + swap_got[rows, :]
        pltpu.make_async_copy(item_sum.at[rows], item_hbm.at[rows], out_sem).start()

    tail = pl.ds(TRI, PACK - TRI)
    part[tail, :] = rhs_rows(1 - row)
    swap_copy(2, tail).start()

    def away_step(i, carry):
        rows = pl.ds(pl.multiple_of(i * 640, 640), 640)
        part[rows, :] = gram_rows(1 - row, rows)
        swap_copy(i, rows).start()
        return carry

    def home_step(i, carry):
        rows = pl.ds(pl.multiple_of(i * 640, 640), 640)
        finish(i, rows, gram_rows(row, rows))
        return carry

    lax.fori_loop(0, 2, away_step, 0)
    finish(2, tail, rhs_rows(row))
    lax.fori_loop(0, 2, home_step, 0)
    w_out.wait()
    take(part, out_sem)
    take(vt_all.at[:, 0:3 * items], v_send.at[0])
    take(vt_all.at[:, 0:3 * items], v_send.at[1])
    take(mqs.at[0:2], m_send)
    take(hop, hop_send)
    take(hop, fwd_send)
    take(rel, rel_send)
    take(got, got_send)
    take(fin, fin_send)
    take(w_all.at[0:count - 1], w_send)
    take(part, x_send)


def half_steps(ratings, mask, vt, count):
    users, items = ratings.shape
    block = users // SIDE
    dma = pltpu.SemaphoreType.DMA
    any_spec = pl.BlockSpec(memory_space=pl.ANY)
    f32, bf16 = jnp.float32, jnp.bfloat16
    return pl.pallas_call(
        als_kernel,
        out_shape=(
            jax.ShapeDtypeStruct((32, WIDTH), f32),
            jax.ShapeDtypeStruct((PACK, items // 2), f32),
        ),
        in_specs=[any_spec, any_spec, any_spec],
        out_specs=(any_spec, any_spec),
        scratch_shapes=[
            pltpu.VMEM((4, block, items), f32),
            pltpu.VMEM((4, block, items), jnp.int32),
            pltpu.VMEM((WIDTH, items), f32),
            pltpu.VMEM((4, SIDE, SIDE, 2, 2, 16, items), bf16),
            pltpu.VMEM((4, 2, 2, SIDE, 16, items), bf16),
            pltpu.VMEM((4, 2, SIDE, 2, 16, 7 * items), bf16),
            pltpu.VMEM((64, 7 * items), bf16),
            pltpu.VMEM((TRI, 7 * items), bf16),
            pltpu.VMEM((TRI, items), f32),
            pltpu.VMEM((PACK, 128), f32),
            pltpu.VMEM((4, PACK, 128), f32),
            pltpu.VMEM((3, 2, HALF, 128), f32),
            pltpu.VMEM((2, HALF, 128), f32),
            pltpu.VMEM((2, 2, HALF, 128), f32),
            pltpu.VMEM((PACK, 128), f32),
            pltpu.VMEM((FULL, 128), f32),
            pltpu.VMEM((128, FULL), f32),
            pltpu.VMEM((2, 3, 16, FULL), f32),
            pltpu.VMEM((WIDTH * ROWS, 128), f32),
            pltpu.VMEM((ROWS, 128), f32),
            pltpu.VMEM((ROWS, 128), f32),
            pltpu.VMEM((32, WIDTH), f32),
            pltpu.VMEM((16, 128), bf16),
            pltpu.VMEM((count, 16, 128), bf16),
            pltpu.VMEM((128, 16 * SIDE * SIDE), f32),
            pltpu.VMEM((64, 32 * count), bf16),
            pltpu.VMEM((PACK, items // 2), f32),
            pltpu.VMEM((PACK, items // 2), f32),
            pltpu.VMEM((PACK, items // 2), f32),
            dma, dma((4,)), dma((2,)), dma((4,)), dma, dma((4,)), dma, dma((4,)), dma, dma((4,)),
            dma, dma((2,)), dma, dma((3,)), dma, dma, dma, dma((4,)), dma, dma, dma((3,)), dma,
            pltpu.SemaphoreType.REGULAR, pltpu.SemaphoreType.REGULAR,
        ],
        compiler_params=pltpu.CompilerParams(
            collective_id=0, has_side_effects=True, vmem_limit_bytes=60 * 1024 * 1024
        ),
    )(ratings, mask, vt)


def solution(mesh):
    block_spec = P(("part", "row"), "col")
    in_specs = (block_spec, block_spec, P(("part", "col"), None))
    out_specs = (P(("part", "row", "col"), None), P(("part", "col", "row"), None))
    count = mesh.shape["col"]

    def local_als(ratings, mask, v_init):
        w_own, packed = half_steps(ratings, mask, v_init.T, count)
        v_own, w_own = solve_items(packed, w_own)
        return w_own, v_own.T

    return jax.shard_map(local_als, mesh=mesh, in_specs=in_specs, out_specs=out_specs, check_vma=False)
```

profile of v0, /device:TPU:1, one launch (start us, length us, event | category | flops | bytes accessed | tf_op | source)
XLA Modules:
  0.0 70.5 jit_solution(17625885835050101185)
XLA Ops:
  0.6 62.8 %shard_map.50 = (f32[32,50]{1,0:T(8,128)}, f32[1344,256]{1,0:T(8,128)}) custom-call(f32[2048,512]{1,0:T(8,128)} %rate_hbm.1, s32[2048,512]{1,0:T(8,128)} %mask_hbm.1, f32[50,512]{1,0:T(8,128)} %bitcast.2), custom_call_target="tpu_custom_call" | custom-call | tf_op jit(solution)/shard_map/pallas_call | solution.py:538
  63.5 6.9 %shard_map.51 = (f32[50,256]{1,0:T(8,128)}, f32[32,50]{1,0:T(8,128)}) custom-call(f32[1344,256]{1,0:T(8,128)} %get-tuple-element.6.g_hbm, f32[32,50]{1,0:T(8,128)} %get-tuple-element.7.w_ref), custom_call_target="tpu_custom_call" | custom-call | tf_op jit(solution)/shard_map/pallas_call | solution.py:123
where the time goes:
time: 70.8 us; the launch traced here: 70.5 us
  Pallas kernels  69.7 us (98%)
  between operations  0.8 us (1%)
    pallas_call x1, Pallas kernels, half_steps(): pl.pallas_call(als_kernel, out_shape=(jax.ShapeDtypeStruct((32, WIDTH), f...  62.8 us
    pallas_call x1, Pallas kernels, solve_items(): pl.pallas_call(item_solve_kernel, out_shape=(jax.ShapeDtypeStruct((WIDTH,...  6.91 us

commit v1 on v0

--- a/solution.py
+++ b/solution.py
@@ -57,12 +57,12 @@
         elif len(groups) * count * rows <= 48 * 8:
             parts = lax.fori_loop(
                 0, first, lambda k, parts: [update(fac, k, accs) for fac, accs in zip(facs, parts)],
-                [panel(here) for here in groups], unroll=2,
+                [panel(here) for here in groups], unroll=4,
             )
         else:
             parts = []
             for here, fac in zip(groups, facs):
-                parts.append(lax.fori_loop(0, first, lambda k, accs: update(fac, k, accs), panel(here), unroll=2))
+                parts.append(lax.fori_loop(0, first, lambda k, accs: update(fac, k, accs), panel(here), unroll=4))
         parts = [list(accs) for accs in parts]
         for c in range(count):
             j = first + c

time: 70.8 us -> 69.7 us (0.984)
  Pallas kernels: 69.7 us -> 68.7 us
where the time goes in v1:
time: 69.7 us; the launch traced here: 69.5 us
  Pallas kernels  68.7 us (99%)
  between operations  0.8 us (1%)
    pallas_call x1, Pallas kernels, half_steps(): pl.pallas_call(als_kernel, out_shape=(jax.ShapeDtypeStruct((32, WIDTH), f...  62.5 us
    pallas_call x1, Pallas kernels, solve_items(): pl.pallas_call(item_solve_kernel, out_shape=(jax.ShapeDtypeStruct((WIDTH,...  6.26 us

profile of v1, /device:TPU:1, one launch (start us, length us, event | category | flops | bytes accessed | tf_op | source)
XLA Modules:
  0.0 69.5 jit_solution(2360831000258483830)
XLA Ops:
  0.6 62.5 %shard_map.50 = (f32[32,50]{1,0:T(8,128)}, f32[1344,256]{1,0:T(8,128)}) custom-call(f32[2048,512]{1,0:T(8,128)} %rate_hbm.1, s32[2048,512]{1,0:T(8,128)} %mask_hbm.1, f32[50,512]{1,0:T(8,128)} %bitcast.2), custom_call_target="tpu_custom_call" | custom-call | tf_op jit(solution)/shard_map/pallas_call | solution.py:538
  63.1 6.3 %shard_map.51 = (f32[50,256]{1,0:T(8,128)}, f32[32,50]{1,0:T(8,128)}) custom-call(f32[1344,256]{1,0:T(8,128)} %get-tuple-element.6.g_hbm, f32[32,50]{1,0:T(8,128)} %get-tuple-element.7.w_ref), custom_call_target="tpu_custom_call" | custom-call | tf_op jit(solution)/shard_map/pallas_call | solution.py:123

commit v2 on v1

--- a/solution.py
+++ b/solution.py
@@ -57,12 +57,12 @@
         elif len(groups) * count * rows <= 48 * 8:
             parts = lax.fori_loop(
                 0, first, lambda k, parts: [update(fac, k, accs) for fac, accs in zip(facs, parts)],
-                [panel(here) for here in groups], unroll=4,
+                [panel(here) for here in groups], unroll=8,
             )
         else:
             parts = []
             for here, fac in zip(groups, facs):
-                parts.append(lax.fori_loop(0, first, lambda k, accs: update(fac, k, accs), panel(here), unroll=4))
+                parts.append(lax.fori_loop(0, first, lambda k, accs: update(fac, k, accs), panel(here), unroll=8))
         parts = [list(accs) for accs in parts]
         for c in range(count):
             j = first + c

time: 69.7 us -> 69.2 us (level)
  no operation moved by 1% of the time
where the time goes in v2:
time: 69.2 us; the launch traced here: 69 us
  Pallas kernels  68.2 us (99%)
  between operations  0.8 us (1%)
    pallas_call x1, Pallas kernels, half_steps(): pl.pallas_call(als_kernel, out_shape=(jax.ShapeDtypeStruct((32, WIDTH), f...  62.2 us
    pallas_call x1, Pallas kernels, solve_items(): pl.pallas_call(item_solve_kernel, out_shape=(jax.ShapeDtypeStruct((WIDTH,...  5.95 us

profile of v2, /device:TPU:1, one launch (start us, length us, event | category | flops | bytes accessed | tf_op | source)
XLA Modules:
  0.0 69.0 jit_solution(12040228279156395325)
XLA Ops:
  0.6 62.2 %shard_map.50 = (f32[32,50]{1,0:T(8,128)}, f32[1344,256]{1,0:T(8,128)}) custom-call(f32[2048,512]{1,0:T(8,128)} %rate_hbm.1, s32[2048,512]{1,0:T(8,128)} %mask_hbm.1, f32[50,512]{1,0:T(8,128)} %bitcast.2), custom_call_target="tpu_custom_call" | custom-call | tf_op jit(solution)/shard_map/pallas_call | solution.py:538
  62.9 5.9 %shard_map.51 = (f32[50,256]{1,0:T(8,128)}, f32[32,50]{1,0:T(8,128)}) custom-call(f32[1344,256]{1,0:T(8,128)} %get-tuple-element.6.g_hbm, f32[32,50]{1,0:T(8,128)} %get-tuple-element.7.w_ref), custom_call_target="tpu_custom_call" | custom-call | tf_op jit(solution)/shard_map/pallas_call | solution.py:123
